TPU v7x, 32 devices: a whole 2x2x4 slice. The times are simulated.
32 devices in a mesh: ep: 4 (over y, core), fsdp: 8 (over z, x).
Axes of the slice: x: 2, y: 2, z: 4, core: 2. Of those that a mesh axis runs over, the one named last changes fastest.
Arguments:
- w_down: float32 [16, 6400, 4096], P('ep', None, 'fsdp'), may hold values from -0.109375 to 0.109375
- router_weight: float32 [4096, 16], P('fsdp', 'ep'), may hold values from -0.09375 to 0.09375
- router_gain: float32 [4096], P('fsdp'), may hold values from 0.25 to 1.75
Outputs:
- serve_down: bfloat16 [16, 6400, 4096], P('ep', 'fsdp')
- scale_down: float32 [16, 6400], P('ep', 'fsdp')
- serve_router: bfloat16 [4096, 16], replicated
All inputs are finite; a program needn't handle non-finite values.
Results may differ from a plain program's by a relative error of at most 0.001.
Values may be sent and summed in bfloat16 or wider, within the bound.
A program may use at most 192 MiB of HBM per device.

v0:
```python
import jax
import jax.numpy as jnp
from jax import lax
from jax.sharding import PartitionSpec as P


def body(w_down, router_weight, router_gain):
    total_down = lax.psum(jnp.sum(w_down * w_down, axis=2), "fsdp")
    scale_down = jnp.sqrt(total_down)
    narrow_down = (w_down / jnp.expand_dims(scale_down, 2)).astype(jnp.bfloat16)
    serve_down = lax.all_to_all(narrow_down, "fsdp", split_axis=1, concat_axis=2, tiled=True)
    scale_down = lax.dynamic_slice_in_dim(
        scale_down, lax.axis_index("fsdp") * serve_down.shape[1], serve_down.shape[1], axis=1
    )
    part_router = (router_weight * router_gain[:, None]).astype(jnp.bfloat16)
    row_router = lax.all_gather(part_router, "fsdp", axis=0, tiled=True)
    serve_router = lax.all_gather(row_router, "ep", axis=1, tiled=True)
    return (serve_down, scale_down, serve_router)


def solution(mesh):
    in_specs = (P("ep", None, "fsdp"), P("fsdp", "ep"), P("fsdp"))
    out_specs = (P("ep", "fsdp", None), P("ep", "fsdp"), P())
    return jax.shard_map(body, mesh=mesh, in_specs=in_specs, out_specs=out_specs, check_vma=False)
```

profile of v0, /device:TPU:0, one launch (start us, length us, event | category | flops | bytes accessed | tf_op | source)
XLA Modules:
  0.0 818.4 jit_solution(10136285089813340323)
XLA Ops:
  7.2 0.0 all-reduce.2.cloned.1.call-start
  7.2 17.4 %multiply_reduce_fusion = f32[4,6400]{1,0:T(4,128)} fusion(f32[4,6400,512]{2,1,0:T(8,128)} %param.3), kind=kLoop, calls=%fused_computation.1 | loop fusion | flops 26188800 | bytes 52531200 | tf_op jit(solution)/shard_map/reduce_sum | solution.py:8
  24.6 0.0 all-reduce.2.cloned.1.call-update
  24.6 72.5 %all-reduce.2.cloned.1.call-done = f32[4,6400]{1,0:T(4,128)} async-done(((f32[4,6400]{1,0:T(4,128)}), f32[4,6400]{1,0:T(4,128)}) %all-reduce.2.cloned.1.call-update) | async-done | bytes 102416 | tf_op jit(solution)/shard_map/psum | solution.py:8
  97.1 0.9 sqrt.3
  98.1 1.1 copy.7
  99.2 0.0 copy-start
  99.2 0.0 copy-start.1
  99.2 58.2 %fusion = bf16[4,6400,512]{2,0,1:T(4,128)(2,1)} fusion(f32[4,6400,512]{2,1,0:T(8,128)} %param.3, f32[4,6400]{0,1:T(8,128)S(1)} %copy.7), kind=kLoop, calls=%fused_computation.2 | loop fusion | flops 26214400 | bytes 78745600 | tf_op jit(solution)/shard_map/convert_element_type | solution.py:10
  157.4 6.5 all-to-all-start
  163.9 0.0 copy-done
  163.9 0.0 copy-done.1
  163.9 583.4 %all_gather.6 = bf16[4096,4]{0,1:T(4,128)(2,1)S(1)} all-gather(bf16[512,4]{0,1:T(4,128)(2,1)S(1)} %multiply_convert_fusion), channel_id=1, replica_groups=mesh['ep'=4,'fsdp'=8] {'fsdp'}, dimensions={0}, use_global_device_ids=true | all-gather | bytes 36864 | tf_op jit(solution)/shard_map/all_gather | solution.py:16
  747.3 5.4 all-gather
  752.8 0.7 reshape.9
  753.4 0.7 constant_dynamic-slice_fusion
  754.1 0.0 all-to-all-done
  754.1 18.2 %copy.9 = bf16[4,800,8,512]{3,2,1,0:T(8,128)(2,1)} copy(bf16[4,800,8,512]{3,0,1,2:T(4,128)(2,1)} %bitcast.1) | data formatting | bytes 52428800 | tf_op jit(solution)/shard_map/all_to_all | solution.py:11
  772.3 39.2 %all_to_all.16 = bf16[4,800,4096]{2,1,0:T(8,128)(2,1)} reshape(bf16[4,800,8,512]{3,2,1,0:T(8,128)(2,1)} %copy.9) | data formatting | bytes 52428800 | tf_op jit(solution)/shard_map/all_to_all | solution.py:11
  (1 shorter events, 0.0 us)
Async XLA Ops:
  7.2 90.0 %all-reduce.2.cloned.1.call-start = ((), (), s32[]{:S(2)}) async-start(), calls=%async_computation.1 | async-start | bytes 204800 | tf_op jit(solution)/shard_map/psum | solution.py:8
  99.2 64.7 %copy-start = (f32[512,4]{0,1:T(4,128)S(1)}, f32[512,4]{0,1:T(4,128)}, u32[]{:S(2)}) copy-start(f32[512,4]{0,1:T(4,128)} %param.4) | copy-start | bytes 24580
  99.2 64.7 %copy-start.1 = (f32[512]{0:T(512)S(1)}, f32[512]{0:T(512)}, u32[]{:S(2)}) copy-start(f32[512]{0:T(512)} %param.5) | copy-start | bytes 6148
  157.4 596.7 %all-to-all-start = ((bf16[4,6400,512]{2,0,1:T(4,128)(2,1)}), bf16[4,6400,512]{2,0,1:T(4,128)(2,1)}, u32[]{:S(2)}, u32[]{:S(2)}) async-start(bf16[4,6400,512]{2,0,1:T(4,128)(2,1)} %fusion), calls=%async_computation | async-start | bytes 52428800 | tf_op jit(solution)/shard_map/all_to_all | solution.py:11
Sparse Core Ops, SparseCore 0:
  24.8 72.3 all-reduce.1
where the time goes:
time: 820 us; the launch traced here: 818 us
  blocking collectives  589 us (72%)
  other arithmetic  75.6 us (9%)
  waiting for transfers between devices  72.5 us (9%)
  local copies, waits for them, and re-layouts  60.8 us (7%)
  between operations  14.1 us (2%)
    all_gather x1, blocking collectives, body(): row_router = lax.all_gather(part_router, 'fsdp', axis=0, tiled=True)  583 us
    psum x1, waiting for transfers between devices, body(): total_down = lax.psum(jnp.sum(w_down * w_down, axis=2), 'fsdp')  72.5 us
    convert_element_type x1, other arithmetic, body(): narrow_down = (w_down / jnp.expand_dims(scale_down, 2)).astype(jnp.bfloat16)  58.2 us
    all_to_all x2, local copies, waits for them, and re-layouts, body(): lax.all_to_all(narrow_down, 'fsdp', split_axis=1, concat_axis=2, tiled=True)  57.4 us
    reduce_sum x1, other arithmetic, body(): total_down = lax.psum(jnp.sum(w_down * w_down, axis=2), 'fsdp')  17.4 us
  transfers between devices with their start and end apart: 2, of which 1 were waited for; matrix products, arithmetic and copies ran while one was open for 0% of the time, Pallas kernels for 0%

commit v1 on v0

--- a/solution.py
+++ b/solution.py
@@ -5,7 +5,7 @@
 
 
 def body(w_down, router_weight, router_gain):
-    total_down = lax.psum(jnp.sum(w_down * w_down, axis=2), "fsdp")
+    total_down = jnp.sum(lax.all_gather(jnp.sum(w_down * w_down, axis=2), "fsdp"), axis=0)
     scale_down = jnp.sqrt(total_down)
     narrow_down = (w_down / jnp.expand_dims(scale_down, 2)).astype(jnp.bfloat16)
     serve_down = lax.all_to_all(narrow_down, "fsdp", split_axis=1, concat_axis=2, tiled=True)

time: 820 us -> 763 us (0.930)
  waiting for transfers between devices: 72.5 us -> 0.01 us
  blocking collectives: 589 us -> 620 us
  between operations: 14.1 us -> 0.71 us
    psum x1 -> x0, waiting for transfers between devices: 72.5 us -> none  [body(): total_down = lax.psum(jnp.sum(w_down * w_down, axis=2), 'fsdp')]
    all_gather x0 -> x1, blocking collectives: none -> 33.9 us  [body(): lax.all_gather(jnp.sum(w_down * w_down, axis=2), 'fsdp')]
    reduce_sum x1 -> x2, other arithmetic: 17.4 us -> 16.9 us  [the longest x1 16.8 us: body(): jnp.sum(w_down * w_down, axis=2)]
  transfers between devices with their start and end apart: 2 -> 1, of which waited for: 1 -> 0; matrix products, arithmetic and copies ran while one was open for 0% -> 0% of each run, Pallas kernels for 0% -> 0%
where the time goes in v1:
time: 763 us; the launch traced here: 762 us
  blocking collectives  620 us (81%)
  other arithmetic  74.8 us (10%)
  local copies, waits for them, and re-layouts  59.9 us (8%)
    all_gather x1, blocking collectives, body(): row_router = lax.all_gather(part_router, 'fsdp', axis=0, tiled=True)  580 us
    convert_element_type x1, other arithmetic, body(): narrow_down = (w_down / jnp.expand_dims(scale_down, 2)).astype(jnp.bfloat16)  57.9 us
    all_to_all x2, local copies, waits for them, and re-layouts, body(): lax.all_to_all(narrow_down, 'fsdp', split_axis=1, concat_axis=2, tiled=True)  57.4 us
    all_gather x1, blocking collectives, body(): lax.all_gather(jnp.sum(w_down * w_down, axis=2), 'fsdp')  33.9 us
    reduce_sum x1, other arithmetic, body(): jnp.sum(w_down * w_down, axis=2)  16.8 us
  transfers between devices with their start and end apart: 1, of which 0 were waited for; matrix products, arithmetic and copies ran while one was open for 0% of the time, Pallas kernels for 0%

profile of v1, /device:TPU:0, one launch (start us, length us, event | category | flops | bytes accessed | tf_op | source)
XLA Modules:
  0.0 761.5 jit_solution(15995414812339284025)
XLA Ops:
  0.6 16.8 %multiply_reduce_fusion = f32[4,6400]{1,0:T(4,128)S(1)} fusion(f32[4,6400,512]{2,1,0:T(8,128)} %param.3), kind=kLoop, calls=%fused_computation.1 | loop fusion | flops 26188800 | bytes 52531200 | tf_op jit(solution)/shard_map/reduce_sum | solution.py:8
  17.4 33.9 %all-gather.1 = f32[8,4,6400]{2,1,0:T(4,128)S(1)} all-gather(f32[1,4,6400]{2,1,0:T(4,128)S(1)} %bitcast.10), channel_id=2, replica_groups=mesh['ep'=4,'fsdp'=8] {'fsdp'}, dimensions={0}, use_global_device_ids=true | all-gather | bytes 921600 | tf_op jit(solution)/shard_map/all_gather | solution.py:8
  51.3 0.1 reduce_sum.19
  51.5 0.1 sqrt.7
  51.5 1.1 copy.7
  52.6 0.0 copy-start
  52.7 0.0 copy-start.1
  52.7 57.9 %fusion = bf16[4,6400,512]{2,0,1:T(4,128)(2,1)} fusion(f32[4,6400,512]{2,1,0:T(8,128)} %param.3, f32[4,6400]{0,1:T(8,128)S(1)} %copy.7), kind=kLoop, calls=%fused_computation.2 | loop fusion | flops 26214400 | bytes 78745600 | tf_op jit(solution)/shard_map/convert_element_type | solution.py:10
  110.6 6.5 all-to-all-start
  117.1 0.0 copy-done
  117.1 0.0 copy-done.1
  117.1 580.2 %all_gather.14 = bf16[4096,4]{0,1:T(4,128)(2,1)S(1)} all-gather(bf16[512,4]{0,1:T(4,128)(2,1)S(1)} %multiply_convert_fusion), channel_id=1, replica_groups=mesh['ep'=4,'fsdp'=8] {'fsdp'}, dimensions={0}, use_global_device_ids=true | all-gather | bytes 36864 | tf_op jit(solution)/shard_map/all_gather | solution.py:16
  697.4 5.4 all-gather.2
  702.8 0.7 reshape.14
  703.5 0.7 constant_dynamic-slice_fusion
  704.1 0.0 all-to-all-done
  704.1 18.2 %copy.9 = bf16[4,800,8,512]{3,2,1,0:T(8,128)(2,1)} copy(bf16[4,800,8,512]{3,0,1,2:T(4,128)(2,1)} %bitcast.2) | data formatting | bytes 52428800 | tf_op jit(solution)/shard_map/all_to_all | solution.py:11
  722.4 39.2 %all_to_all.16 = bf16[4,800,4096]{2,1,0:T(8,128)(2,1)} reshape(bf16[4,800,8,512]{3,2,1,0:T(8,128)(2,1)} %copy.9) | data formatting | bytes 52428800 | tf_op jit(solution)/shard_map/all_to_all | solution.py:11
  (1 shorter events, 0.0 us)
Async XLA Ops:
  52.6 64.4 %copy-start = (f32[512,4]{0,1:T(4,128)S(1)}, f32[512,4]{0,1:T(4,128)}, u32[]{:S(2)}) copy-start(f32[512,4]{0,1:T(4,128)} %param.4) | copy-start | bytes 24580
  52.7 64.4 %copy-start.1 = (f32[512]{0:T(512)S(1)}, f32[512]{0:T(512)}, u32[]{:S(2)}) copy-start(f32[512]{0:T(512)} %param.5) | copy-start | bytes 6148
  110.6 593.6 %all-to-all-start = ((bf16[4,6400,512]{2,0,1:T(4,128)(2,1)}), bf16[4,6400,512]{2,0,1:T(4,128)(2,1)}, u32[]{:S(2)}, u32[]{:S(2)}) async-start(bf16[4,6400,512]{2,0,1:T(4,128)(2,1)} %fusion), calls=%async_computation | async-start | bytes 52428800 | tf_op jit(solution)/shard_map/all_to_all | solution.py:11

commit v2 on v0

--- a/solution.py
+++ b/solution.py
@@ -8,7 +8,12 @@
     total_down = lax.psum(jnp.sum(w_down * w_down, axis=2), "fsdp")
     scale_down = jnp.sqrt(total_down)
     narrow_down = (w_down / jnp.expand_dims(scale_down, 2)).astype(jnp.bfloat16)
-    serve_down = lax.all_to_all(narrow_down, "fsdp", split_axis=1, concat_axis=2, tiled=True)
+    serve_down = jnp.concatenate(
+        lax.all_to_all(
+            jnp.stack(jnp.split(narrow_down, lax.axis_size("fsdp"), axis=1)), "fsdp", 0, 0
+        ),
+        axis=2,
+    )
     scale_down = lax.dynamic_slice_in_dim(
         scale_down, lax.axis_index("fsdp") * serve_down.shape[1], serve_down.shape[1], axis=1
     )

time: 820 us -> 777 us (0.948)
  other arithmetic: 75.6 us -> 43.5 us
  local copies, waits for them, and re-layouts: 60.8 us -> 50.8 us
    all_to_all x2 -> x0, local copies, waits for them, and re-layouts: 57.4 us -> none  [body(): lax.all_to_all(narrow_down, 'fsdp', split_axis=1, concat_axis=2, tiled=True)]
    convert_element_type x1, other arithmetic: 58.2 us -> 26.1 us  [body(): narrow_down = (w_down / jnp.expand_dims(scale_down, 2)).astype(jnp.bfloat16)]
    unnamed x5 -> x12, local copies, waits for them, and re-layouts: 0.7 us -> 27.5 us
    reshape x0 -> x1, local copies, waits for them, and re-layouts: none -> 17.9 us  [body(): jnp.concatenate(lax.all_to_all(jnp.stack(jnp.split(narrow_down, lax.axis_...]
where the time goes in v2:
time: 777 us; the launch traced here: 776 us
  blocking collectives  589 us (76%)
  waiting for transfers between devices  72.5 us (9%)
  local copies, waits for them, and re-layouts  50.8 us (7%)
  other arithmetic  43.5 us (6%)
  between operations  14.1 us (2%)
    all_gather x1, blocking collectives, body(): row_router = lax.all_gather(part_router, 'fsdp', axis=0, tiled=True)  583 us
    psum x1, waiting for transfers between devices, body(): total_down = lax.psum(jnp.sum(w_down * w_down, axis=2), 'fsdp')  72.5 us
    unnamed x12, local copies, waits for them, and re-layouts  27.5 us
    convert_element_type x1, other arithmetic, body(): narrow_down = (w_down / jnp.expand_dims(scale_down, 2)).astype(jnp.bfloat16)  26.1 us
    reshape x1, local copies, waits for them, and re-layouts, body(): jnp.concatenate(lax.all_to_all(jnp.stack(jnp.split(narrow_down, lax.axis_...  17.9 us
    reduce_sum x1, other arithmetic, body(): total_down = lax.psum(jnp.sum(w_down * w_down, axis=2), 'fsdp')  17.4 us
  transfers between devices with their start and end apart: 2, of which 1 were waited for; matrix products, arithmetic and copies ran while one was open for 0% of the time, Pallas kernels for 0%

profile of v2, /device:TPU:0, one launch (start us, length us, event | category | flops | bytes accessed | tf_op | source)
XLA Modules:
  0.0 776.4 jit_solution(16197063411485344824)
XLA Ops:
  7.2 0.0 all-reduce.2.cloned.1.call-start
  7.2 17.4 %multiply_reduce_fusion = f32[4,6400]{1,0:T(4,128)} fusion(f32[4,6400,512]{2,1,0:T(8,128)} %param.3), kind=kLoop, calls=%fused_computation.1 | loop fusion | flops 26188800 | bytes 52531200 | tf_op jit(solution)/shard_map/reduce_sum | solution.py:8
  24.6 0.0 all-reduce.2.cloned.1.call-update
  24.6 72.5 %all-reduce.2.cloned.1.call-done = f32[4,6400]{1,0:T(4,128)} async-done(((f32[4,6400]{1,0:T(4,128)}), f32[4,6400]{1,0:T(4,128)}) %all-reduce.2.cloned.1.call-update) | async-done | bytes 102416 | tf_op jit(solution)/shard_map/psum | solution.py:8
  97.1 0.9 sqrt.3
  98.1 26.1 %divide_convert_fusion = bf16[4,6400,512]{2,1,0:T(8,128)(2,1)} fusion(f32[4,6400,512]{2,1,0:T(8,128)} %param.3, f32[4,6400]{1,0:T(4,128)S(1)} %sqrt.3), kind=kLoop, calls=%fused_computation | loop fusion | flops 26214400 | bytes 78745600 | tf_op jit(solution)/shard_map/convert_element_type | solution.py:10
  124.2 3.8 fusion.7
  128.0 3.8 fusion.6
  131.9 3.8 fusion.5
  135.7 3.8 fusion.4
  139.5 3.9 fusion.3
  143.4 3.8 fusion.2
  147.2 3.8 fusion.1
  151.0 3.8 fusion
  154.8 0.0 copy-start
  154.8 0.0 copy-start.1
  154.8 6.6 all-to-all-start
  161.4 0.0 copy-done
  161.5 0.0 copy-done.1
  161.5 583.4 %all_gather.6 = bf16[4096,4]{0,1:T(4,128)(2,1)S(1)} all-gather(bf16[512,4]{0,1:T(4,128)(2,1)S(1)} %multiply_convert_fusion), channel_id=1, replica_groups=mesh['ep'=4,'fsdp'=8] {'fsdp'}, dimensions={0}, use_global_device_ids=true | all-gather | bytes 36864 | tf_op jit(solution)/shard_map/all_gather | solution.py:21
  744.9 5.4 all-gather
  750.3 0.7 reshape.17
  751.0 0.7 constant_dynamic-slice_fusion
  751.7 0.0 all-to-all-done
  751.7 17.9 %copy.8 = bf16[8,4,100,8,512]{4,3,0,2,1:T(8,128)(2,1)} copy(bf16[8,4,100,8,512]{4,3,2,1,0:T(8,128)(2,1)} %bitcast.13) | data formatting | bytes 52428800 | tf_op jit(solution)/shard_map/reshape | solution.py:11
  (1 shorter events, 0.0 us)
Async XLA Ops:
  7.2 90.0 %all-reduce.2.cloned.1.call-start = ((), (), s32[]{:S(2)}) async-start(), calls=%async_computation.1 | async-start | bytes 204800 | tf_op jit(solution)/shard_map/psum | solution.py:8
  154.8 6.6 copy-start
  154.8 6.6 copy-start.1
  154.8 596.9 %all-to-all-start = ((bf16[8,4,800,512]{3,2,1,0:T(8,128)(2,1)}), bf16[8,4,800,512]{3,2,1,0:T(8,128)(2,1)}, u32[]{:S(2)}, u32[]{:S(2)}) async-start(bf16[8,4,800,512]{3,2,1,0:T(8,128)(2,1)} %fusion), calls=%async_computation | async-start | bytes 52428800 | tf_op jit(solution)/shard_map/all_to_all | solution.py:12
Sparse Core Ops, SparseCore 0:
  24.8 72.3 all-reduce.1
